TPU v7x, 256 devices: a whole 4x4x8 slice. The times are simulated.
256 devices in a mesh: ctx: 64 (over y_hi, z, x), tp: 4 (over y_lo, core).
Axes of the slice: x: 4, y: 4 (y_hi: 2, y_lo: 2; y = y_hi * 2 + y_lo), z: 8, core: 2. Of those that a mesh axis runs over, the one named last changes fastest.
Arguments:
- gate_branch: bfloat16 [4096, 16384], P('tp', 'ctx'), may hold values from -6 to 6
- key_branch: bfloat16 [4096, 16384], P('tp', 'ctx'), may hold values from -6 to 6
- value_branch: bfloat16 [4096, 16384], P('tp', 'ctx'), may hold values from -6 to 6
- long_filter: bfloat16 [4096, 16384], P('tp', 'ctx'), may hold values from -0.046875 to 0.046875
- skip_gain: float32 [4096], P('tp'), may hold values from 0.25 to 2
- out_weight: bfloat16 [4096, 4096], P(None, 'tp'), may hold values from -0.09375 to 0.09375
Outputs:
- mixer_out: bfloat16 [4096, 16384], P('tp', 'ctx')
All inputs are finite; a program needn't handle non-finite values.
Results may differ from a plain program's by a relative error of at most 0.013.
Values may be sent and summed in bfloat16 or wider, within the bound.
A program may use at most 64 MiB of HBM per device.

v0:
```python
import math

import jax
import jax.numpy as jnp
from jax import lax
from jax.sharding import PartitionSpec as P

triple = lax.Precision.HIGH


def split_up(shard, dim, size):
    before, after = (shard.shape[:dim], shard.shape[dim + 1 :])
    return jnp.moveaxis(shard.reshape(*before, size, -1, *after), dim, 0)


def summed_on_arrival(shard, axis, dim):
    size = lax.axis_size(axis)
    tiles = lax.all_to_all(split_up(shard, dim, size), axis, 0, 0, tiled=True)
    return jnp.sum(tiles.astype(jnp.float32), axis=0)


def angle_table(height, breadth, period):
    product = lax.broadcasted_iota(jnp.int32, (height, breadth), 0) * lax.broadcasted_iota(
        jnp.int32, (height, breadth), 1
    )
    angle = (product % period).astype(jnp.float32) * (2.0 * math.pi / period)
    return (jnp.cos(angle), jnp.sin(angle))


def causal_conv(mixed_cols, filter_cols):
    channels, length = mixed_cols.shape
    inner = length // 64
    total = 128 * inner
    cos_one, sin_one = angle_table(128, 64, 128)
    cos_twist, sin_twist = angle_table(128, inner, total)
    cos_two, sin_two = angle_table(inner, inner, inner)

    def right_mul(left, table):
        return jnp.einsum("kcb,bd->kcd", left, table, precision=triple)

    def forward(signal):
        grid = signal.astype(jnp.float32).reshape(channels, 64, inner)
        first_real = jnp.einsum("ca,kab->kcb", cos_one, grid, precision=triple)
        first_imag = -jnp.einsum("ca,kab->kcb", sin_one, grid, precision=triple)
        turned_real = first_real * cos_twist + first_imag * sin_twist
        turned_imag = first_imag * cos_twist - first_real * sin_twist
        spec_real = right_mul(turned_real, cos_two) + right_mul(turned_imag, sin_two)
        spec_imag = right_mul(turned_imag, cos_two) - right_mul(turned_real, sin_two)
        return (spec_real, spec_imag)

    left_real, left_imag = forward(mixed_cols)
    right_real, right_imag = forward(filter_cols)
    prod_real = left_real * right_real - left_imag * right_imag
    prod_imag = left_real * right_imag + left_imag * right_real
    back_real = right_mul(prod_real, cos_two) - right_mul(prod_imag, sin_two)
    back_imag = right_mul(prod_imag, cos_two) + right_mul(prod_real, sin_two)
    untwist_real = back_real * cos_twist - back_imag * sin_twist
    untwist_imag = back_imag * cos_twist + back_real * sin_twist
    signal = jnp.einsum("ca,kcb->kab", cos_one, untwist_real, precision=triple) - jnp.einsum(
        "ca,kcb->kab", sin_one, untwist_imag, precision=triple
    )
    return (signal / total).reshape(channels, length)


def body(gate_branch, key_branch, value_branch, long_filter, skip_gain, out_weight):
    mixed = (key_branch.astype(jnp.float32) * value_branch.astype(jnp.float32)).astype(jnp.bfloat16)
    mixed_cols, filter_cols = (
        lax.all_to_all(mixed, "ctx", split_axis=0, concat_axis=1, tiled=True),
        lax.all_to_all(long_filter, "ctx", split_axis=0, concat_axis=1, tiled=True),
    )
    conv_out = causal_conv(mixed_cols, filter_cols).astype(jnp.bfloat16)
    returned = lax.all_to_all(conv_out, "ctx", split_axis=1, concat_axis=0, tiled=True)
    gated = gate_branch.astype(jnp.float32) * (
        returned.astype(jnp.float32) + skip_gain[:, None] * mixed.astype(jnp.float32)
    )
    gated = gated.astype(jnp.bfloat16)
    output = summed_on_arrival(
        jnp.dot(out_weight, gated, preferred_element_type=jnp.float32).astype(jnp.bfloat16), "tp", 0
    )
    return output.astype(jnp.bfloat16)


def solution(mesh):
    placed = (
        P("tp", "ctx"),
        P("tp", "ctx"),
        P("tp", "ctx"),
        P("tp", "ctx"),
        P("tp"),
        P(None, "tp"),
    )
    return jax.shard_map(
        body, mesh=mesh, in_specs=placed, out_specs=P("tp", "ctx"), check_vma=False
    )
```

profile of v0, /device:TPU:1, one launch (start us, length us, event | category | flops | bytes accessed | tf_op | source)
XLA Modules:
  0.0 147.0 jit_solution(1156221277140644754)
XLA Ops:
  0.0 15.2 %all-to-all-start.1 = ((bf16[64,16,256]{2,1,0:T(8,128)(2,1)}), bf16[64,16,256]{2,1,0:T(8,128)(2,1)S(1)}, u32[]{:S(2)}, u32[]{:S(2)}) async-start(bf16[64,16,256]{2,1,0:T(8,128)(2,1)} %bitcast.117), calls=%async_computation.1 | async-start | bytes 1048576 | tf_op jit(solution)/shard_map/all_to_all | solution.py:69
  17.6 15.3 %all-to-all-done.1 = bf16[64,16,256]{2,1,0:T(8,128)(2,1)S(1)} async-done(((bf16[64,16,256]{2,1,0:T(8,128)(2,1)}), bf16[64,16,256]{2,1,0:T(8,128)(2,1)S(1)}, u32[]{:S(2)}, u32[]{:S(2)}) %all-to-all-start.1) | async-done | bytes 524320 | tf_op jit(solution)/shard_map/all_to_all | solution.py:69
  32.9 7.0 %all-to-all-start = ((bf16[64,16,256]{2,1,0:T(8,128)(2,1)}), bf16[64,16,256]{2,1,0:T(8,128)(2,1)S(1)}, u32[]{:S(2)}, u32[]{:S(2)}) async-start(bf16[64,16,256]{2,1,0:T(8,128)(2,1)} %bitcast), calls=%async_computation | async-start | bytes 1048576 | tf_op jit(solution)/shard_map/all_to_all | solution.py:68
  41.7 3.5 %fusion = f32[16,128,256]{2,1,0:T(8,128)} fusion(f32[128,16,256]{2,0,1:T(8,128)S(1)} %fusion.44, f32[128,16,256]{2,0,1:T(8,128)S(1)} %fusion.42, f32[128,256]{1,0:T(8,128)S(1)} %copy-done.4, f32[128,256]{1,0:T(8,128)S(1)} %copy.38), kind=kOutput, calls=%fused_computation.2 | convolution fusion | flops 808321024 | bytes 6553600 | tf_op jit(solution)/shard_map/kcb,bd->kcd/dot_general | solution.py:39
  45.3 3.5 %fusion.2 = f32[16,128,256]{2,1,0:T(8,128)} fusion(f32[128,16,256]{2,0,1:T(8,128)S(1)} %fusion.44, f32[128,16,256]{2,0,1:T(8,128)S(1)} %fusion.42, f32[128,256]{1,0:T(8,128)S(1)} %copy-done.4, f32[128,256]{1,0:T(8,128)S(1)} %copy.38), kind=kOutput, calls=%fused_computation.4 | convolution fusion | flops 808321024 | bytes 6553600 | tf_op jit(solution)/shard_map/kcb,bd->kcd/dot_general | solution.py:39
  48.8 7.4 %all-to-all-done = bf16[64,16,256]{2,1,0:T(8,128)(2,1)S(1)} async-done(((bf16[64,16,256]{2,1,0:T(8,128)(2,1)}), bf16[64,16,256]{2,1,0:T(8,128)(2,1)S(1)}, u32[]{:S(2)}, u32[]{:S(2)}) %all-to-all-start) | async-done | bytes 524320 | tf_op jit(solution)/shard_map/all_to_all | solution.py:68
  56.2 1.0 fusion.46
  57.2 1.0 fusion.48
  58.3 2.8 %fusion.58 = f32[16,128,256]{2,1,0:T(8,128)S(1)} fusion(f32[16,256,128]{2,1,0:T(8,128)S(1)} %fusion.48, f32[16,256,128]{2,1,0:T(8,128)S(1)} %fusion.46, f32[128,256]{0,1:T(8,128)S(1)} %get-tuple-element.7, f32[128,256]{0,1:T(8,128)S(1)} %get-tuple-element.8), kind=kOutput, calls=%fused_computation.59 | convolution fusion | flops 808321024 | bytes 6553600 | tf_op jit(solution)/shard_map/kcb,bd->kcd/dot_general | solution.py:39
  61.1 3.0 %fusion.54 = f32[16,128,256]{2,1,0:T(8,128)S(1)} fusion(f32[16,256,128]{2,1,0:T(8,128)S(1)} %fusion.48, f32[16,256,128]{2,1,0:T(8,128)S(1)} %fusion.46, f32[128,256]{0,1:T(8,128)S(1)} %get-tuple-element.7, f32[128,256]{0,1:T(8,128)S(1)} %get-tuple-element.8), kind=kOutput, calls=%fused_computation.58 | convolution fusion | flops 808321024 | bytes 6553600 | tf_op jit(solution)/shard_map/kcb,bd->kcd/dot_general | solution.py:39
  64.2 2.2 %fusion.21 = f32[16,128,256]{2,1,0:T(8,128)S(1)} fusion(f32[16,128,256]{2,1,0:T(8,128)S(1)} %copy-done.3, f32[128,16,256]{2,0,1:T(8,128)S(1)} %copy-done.1, f32[128,16,256]{2,0,1:T(8,128)S(1)} %fusion.42, f32[128,256]{1,0:T(8,128)S(1)} %copy-done.5, f32[128,256]{1,0:T(8,128)S(1)} %copy.38), kind=kOutput, calls=%fused_computation.29 | convolution fusion | flops 808845312 | bytes 8650752 | tf_op jit(solution)/shard_map/kcb,bd->kcd/dot_general | solution.py:39
  66.4 2.2 %fusion.18 = f32[16,128,256]{2,1,0:T(8,128)S(1)} fusion(f32[16,128,256]{2,1,0:T(8,128)S(1)} %copy-done.2, f32[128,16,256]{2,0,1:T(8,128)S(1)} %copy-done.1, f32[128,16,256]{2,0,1:T(8,128)S(1)} %fusion.42, f32[128,256]{1,0:T(8,128)S(1)} %copy-done.5, f32[128,256]{1,0:T(8,128)S(1)} %copy.38), kind=kOutput, calls=%fused_computation.28 | convolution fusion | flops 808845312 | bytes 8650752 | tf_op jit(solution)/shard_map/kcb,bd->kcd/dot_general | solution.py:39
  68.6 2.9 %convolution_add_fusion.1 = f32[16,128,256]{2,1,0:T(8,128)S(1)} fusion(f32[16,128,256]{2,1,0:T(8,128)S(1)} %fusion.58, f32[16,256,128]{2,1,0:T(8,128)S(1)} %fusion.48, f32[16,256,128]{2,1,0:T(8,128)S(1)} %fusion.46, f32[128,256]{0,1:T(8,128)S(1)} %get-tuple-element.7, f32[128,256]{0,1:T(8,128)S(1)} %get-tuple-element.8), kind=kOutput, calls=%fused_computation.33 | convolution fusion | flops 808845312 | bytes 8650752 | tf_op jit(solution)/shard_map/kcb,bd->kcd/dot_general | solution.py:39
  71.5 3.3 %multiply_add_fusion = (f32[16,128,256]{2,1,0:T(8,128)S(1)}, f32[16,128,256]{2,1,0:T(8,128)S(1)}) fusion(f32[16,128,256]{2,1,0:T(8,128)S(1)} %fusion.18, f32[16,128,256]{2,1,0:T(8,128)S(1)} %convolution_add_fusion.1, f32[16,128,256]{2,1,0:T(8,128)S(1)} %fusion.21, f32[16,128,256]{2,1,0:T(8,128)S(1)} %fusion.54, f32[16,256,128]{2,1,0:T(8,128)S(1)} %fusion.48, ...), kind=kOutput, calls=%fused_computation.24 | convolution fusion | flops 811991040 | bytes 17039360 | tf_op jit(solution)/shard_map/kcb,bd->kcd/dot_general | solution.py:39
  74.8 2.4 %fusion.69 = f32[16,128,256]{1,2,0:T(8,128)S(1)} fusion(f32[16,128,256]{2,1,0:T(8,128)S(1)} %get-tuple-element.5), kind=kOutput, calls=%fused_computation.72 | convolution fusion | flops 806223872 | bytes 4194304 | tf_op jit(solution)/shard_map/kcb,bd->kcd/dot_general | solution.py:39
  77.2 2.0 %fusion.71 = f32[16,128,256]{1,2,0:T(8,128)S(1)} fusion(f32[16,128,256]{2,1,0:T(8,128)S(1)} %get-tuple-element.6), kind=kOutput, calls=%fused_computation.74 | convolution fusion | flops 806223872 | bytes 4194304 | tf_op jit(solution)/shard_map/kcb,bd->kcd/dot_general | solution.py:39
  79.2 2.1 %convolution_add_fusion = f32[16,128,256]{1,2,0:T(8,128)S(1)} fusion(f32[16,128,256]{1,2,0:T(8,128)S(1)} %fusion.69, f32[16,128,256]{2,1,0:T(8,128)S(1)} %get-tuple-element.6), kind=kOutput, calls=%fused_computation.30 | convolution fusion | flops 806748160 | bytes 6291456 | tf_op jit(solution)/shard_map/kcb,bd->kcd/dot_general | solution.py:39
  81.3 2.1 %convolution_subtract_fusion = f32[16,128,256]{1,2,0:T(8,128)S(1)} fusion(f32[16,128,256]{1,2,0:T(8,128)S(1)} %fusion.71, f32[16,128,256]{2,1,0:T(8,128)S(1)} %get-tuple-element.5), kind=kOutput, calls=%fused_computation.31 | convolution fusion | flops 806748160 | bytes 6291456 | tf_op jit(solution)/shard_map/kcb,bd->kcd/dot_general | solution.py:39
  83.4 1.5 %fusion.10 = f32[16,256,64]{1,2,0:T(8,128)S(1)} fusion(f32[16,128,256]{1,2,0:T(8,128)S(1)} %convolution_subtract_fusion, f32[16,128,256]{1,2,0:T(8,128)S(1)} %convolution_add_fusion, f32[128,256]{0,1:T(8,128)S(1)} %get-tuple-element.7, f32[128,256]{0,1:T(8,128)S(1)} %get-tuple-element.8), kind=kOutput, calls=%fused_computation.16 | convolution fusion | flops 203014144 | bytes 5505024 | tf_op jit(solution)/shard_map/ca,kcb->kab/dot_general | solution.py:59
  84.9 1.5 %fusion.33 = bf16[16,64,256]{2,1,0:T(8,128)(2,1)S(1)} fusion(f32[16,256,64]{1,2,0:T(8,128)S(1)} %fusion.10, f32[16,128,256]{1,2,0:T(8,128)S(1)} %convolution_add_fusion, f32[16,128,256]{1,2,0:T(8,128)S(1)} %convolution_subtract_fusion, f32[128,256]{0,1:T(8,128)S(1)} %get-tuple-element.7, f32[128,256]{0,1:T(8,128)S(1)} %get-tuple-element.8), kind=kOutput, calls=%fused_computation.37 | convolution fusion | flops 203800576 | bytes 6029312 | tf_op jit(solution)/shard_map/ca,kcb->kab/dot_general | solution.py:59
  86.8 23.2 %all_to_all.47 = bf16[16,64,256]{2,0,1:T(8,128)(2,1)S(1)} all-to-all(bf16[16,64,256]{2,0,1:T(8,128)(2,1)S(1)} %copy.48), channel_id=1, replica_groups=mesh['ctx'=64,'tp'=4] {'ctx'}, dimensions={1} | all-to-all | bytes 1048576 | tf_op jit(solution)/shard_map/all_to_all | solution.py:72
  110.0 1.4 fusion.37
  111.4 2.4 %convolution_convert_fusion = bf16[256,4096]{1,0:T(8,128)(2,1)S(1)} fusion(bf16[1024,256]{1,0:T(8,128)(2,1)S(1)} %fusion.37, bf16[4096,1024]{1,0:T(8,128)(2,1)S(1)} %bitcast.119), kind=kOutput, calls=%fused_computation | convolution fusion | flops 2148532224 | bytes 11010048 | tf_op jit(solution)/shard_map/dot_general | solution.py:78
  114.0 31.4 %all_to_all.48 = bf16[4,1024,256]{1,2,0:T(8,128)(2,1)S(1)} all-to-all(bf16[4,1024,256]{1,2,0:T(8,128)(2,1)S(1)} %bitcast.115), channel_id=1, replica_groups=mesh['ctx'=64,'tp'=4] {'tp'}, dimensions={0} | all-to-all | bytes 4194304 | tf_op jit(solution)/shard_map/all_to_all | solution.py:18
  (35 shorter events, 6.1 us)
Async XLA Ops:
  0.0 16.6 %copy-start.7 = (bf16[1024,256]{1,0:T(8,128)(2,1)S(1)}, bf16[1024,256]{1,0:T(8,128)(2,1)}, u32[]{:S(2)}) copy-start(bf16[1024,256]{1,0:T(8,128)(2,1)} %param.7) | copy-start | bytes 1572868
  0.0 16.6 %copy-start.6 = (bf16[1024,256]{1,0:T(8,128)(2,1)S(1)}, bf16[1024,256]{1,0:T(8,128)(2,1)}, u32[]{:S(2)}) copy-start(bf16[1024,256]{1,0:T(8,128)(2,1)} %param.8) | copy-start | bytes 1572868
  0.0 32.9 %all-to-all-start.1 = ((bf16[64,16,256]{2,1,0:T(8,128)(2,1)}), bf16[64,16,256]{2,1,0:T(8,128)(2,1)S(1)}, u32[]{:S(2)}, u32[]{:S(2)}) async-start(bf16[64,16,256]{2,1,0:T(8,128)(2,1)} %bitcast.117), calls=%async_computation.1 | async-start | bytes 1048576 | tf_op jit(solution)/shard_map/all_to_all | solution.py:69
  32.9 23.2 %all-to-all-start = ((bf16[64,16,256]{2,1,0:T(8,128)(2,1)}), bf16[64,16,256]{2,1,0:T(8,128)(2,1)S(1)}, u32[]{:S(2)}, u32[]{:S(2)}) async-start(bf16[64,16,256]{2,1,0:T(8,128)(2,1)} %bitcast), calls=%async_computation | async-start | bytes 1048576 | tf_op jit(solution)/shard_map/all_to_all | solution.py:68
  39.9 1.8 %copy-start.4 = (f32[128,256]{1,0:T(8,128)S(1)}, f32[128,256]{1,0:T(8,128)}, u32[]{:S(2)}) copy-start(f32[128,256]{1,0:T(8,128)} %copy.39) | copy-start | bytes 393220
  41.7 3.6 %copy-start = (f32[128,16,256]{2,0,1:T(8,128)}, f32[128,16,256]{2,0,1:T(8,128)S(1)}, u32[]{:S(2)}) copy-start(f32[128,16,256]{2,0,1:T(8,128)S(1)} %fusion.44) | copy-start | bytes 6291460
  61.1 3.1 %copy-start.1 = (f32[128,16,256]{2,0,1:T(8,128)S(1)}, f32[128,16,256]{2,0,1:T(8,128)}, u32[]{:S(2)}) copy-start(f32[128,16,256]{2,0,1:T(8,128)} %copy-done) | copy-start | bytes 6291460
  61.1 3.1 %copy-start.3 = (f32[16,128,256]{2,1,0:T(8,128)S(1)}, f32[16,128,256]{2,1,0:T(8,128)}, u32[]{:S(2)}) copy-start(f32[16,128,256]{2,1,0:T(8,128)} %fusion) | copy-start | bytes 6291460
  61.1 3.1 %copy-start.5 = (f32[128,256]{1,0:T(8,128)S(1)}, f32[128,256]{1,0:T(8,128)}, u32[]{:S(2)}) copy-start(f32[128,256]{1,0:T(8,128)} %copy.39) | copy-start | bytes 393220
  64.2 2.2 %copy-start.2 = (f32[16,128,256]{2,1,0:T(8,128)S(1)}, f32[16,128,256]{2,1,0:T(8,128)}, u32[]{:S(2)}) copy-start(f32[16,128,256]{2,1,0:T(8,128)} %fusion.2) | copy-start | bytes 6291460
  81.3 30.1 %slice-start = ((s8[8388608]{0:T(1024)(128)(4,1)}), s8[4194304]{0:T(1024)(128)(4,1)S(1)}, s32[]{:S(2)}) async-start(s8[8388608]{0:T(1024)(128)(4,1)} %bitcast.118), calls=%async_computation.4 | async-start | bytes 8388608
  83.4 28.0 %slice-start.1 = ((s8[8388608]{0:T(1024)(128)(4,1)}), s8[4194304]{0:T(1024)(128)(4,1)S(1)}, s32[]{:S(2)}) async-start(s8[8388608]{0:T(1024)(128)(4,1)} %bitcast.118), calls=%async_computation.5 | async-start | bytes 8388608
  86.5 23.5 %copy-start.8 = (bf16[1024,256]{1,0:T(8,128)(2,1)S(1)}, bf16[1024,256]{1,0:T(8,128)(2,1)}, u32[]{:S(2)}) copy-start(bf16[1024,256]{1,0:T(8,128)(2,1)} %param.6) | copy-start | bytes 1572868
  86.5 23.5 %copy-start.9 = (f32[1024]{0:T(1024)S(1)}, f32[1024]{0:T(1024)}, u32[]{:S(2)}) copy-start(f32[1024]{0:T(1024)} %param.10) | copy-start | bytes 12292
where the time goes:
time: 150 us; the launch traced here: 147 us
  blocking collectives  54.6 us (36%)
  matrix products  41.4 us (28%)
  waiting for transfers between devices  22.7 us (15%)
  starting transfers between devices  22.2 us (15%)
  other arithmetic  3.27 us (2%)
  local copies, waits for them, and re-layouts  2.39 us (2%)
    dot_general x12, matrix products, right_mul(): return jnp.einsum('kcb,bd->kcd', left, table, precision=triple)  32 us
    all_to_all x1, blocking collectives, summed_on_arrival(): tiles = lax.all_to_all(split_up(shard, dim, size), axis, 0, 0, tiled=True)  31.4 us
    all_to_all x1, blocking collectives, body(): lax.all_to_all(conv_out, 'ctx', split_axis=1, concat_axis=0, tiled=True)  23.2 us
    all_to_all x1, waiting for transfers between devices, body(): lax.all_to_all(long_filter, 'ctx', split_axis=0, concat_axis=1, tiled=True)  15.3 us
    all_to_all x1, starting transfers between devices, body(): lax.all_to_all(long_filter, 'ctx', split_axis=0, concat_axis=1, tiled=True)  15.2 us
    all_to_all x1, waiting for transfers between devices, body(): lax.all_to_all(mixed, 'ctx', split_axis=0, concat_axis=1, tiled=True)  7.36 us
    all_to_all x1, starting transfers between devices, body(): lax.all_to_all(mixed, 'ctx', split_axis=0, concat_axis=1, tiled=True)  6.97 us
  transfers between devices with their start and end apart: 2, of which 2 were waited for; matrix products, arithmetic and copies ran while one was open for 8% of the time, Pallas kernels for 0%

commit v1 on v0

v1 whole, which is shorter than its diff:
```python
import functools

import jax
import jax.numpy as jnp
import numpy as np
from jax import lax
from jax.experimental import pallas as pl
from jax.experimental.pallas import tpu as pltpu
from jax.sharding import PartitionSpec as P

MESH = pl.DeviceIdType.MESH
CTX = 64
TP = 4
BASE = 128
CHUNKS = 2
GROUP = 8


def tables():
    index = np.arange(BASE)
    first = np.exp(2j * np.pi * np.outer(index + 0.25, index) / BASE)
    twist = np.exp(2j * np.pi * np.outer(index + 0.25, index) / BASE**2)
    second = np.exp(2j * np.pi * np.outer(index, index) / BASE)
    back = first.T / BASE**2
    low = lambda table: jnp.asarray(table, jnp.bfloat16)
    return (
        low(np.concatenate([first.real, first.imag], 0)),
        low(np.block([[second.real, second.imag], [-second.imag, second.real]])),
        low(np.block([[second.real, -second.imag], [second.imag, second.real]])),
        low(np.concatenate([back.real, back.imag], 1)),
        jnp.asarray(np.stack([twist.real, twist.imag]), jnp.float32),
    )


def peer(me, offset):
    high, z, x = me // 32, (me // 4) % 8, me % 4
    return (
        ((high + offset // 32) % 2) * 32
        + ((z + (offset // 4) % 8) % 8) * 4
        + (x + offset % 4) % 4
    )


def dot(left, right):
    return jnp.dot(left, right, preferred_element_type=jnp.float32)


def kernel(
    gate_hbm,
    key_hbm,
    value_hbm,
    filter_hbm,
    skip_ref,
    weight_hbm,
    first_ref,
    second_ref,
    second_back_ref,
    first_back_ref,
    twist_ref,
    out_ref,
    gate,
    key,
    value,
    taps,
    weight,
    mixed,
    skipped,
    in_mixed,
    in_taps,
    stage_mixed,
    stage_taps,
    stage_out,
    back_send,
    back_recv,
    gated,
    core_send,
    core_recv,
    keep,
    y_send,
    y_recv,
    load_sem,
    in_send_sem,
    in_recv_sem,
    back_send_sem,
    back_recv_sem,
    core_send_sem,
    core_recv_sem,
    y_send_sem,
    y_recv_sem,
):
    me, tp = lax.axis_index("ctx"), lax.axis_index("tp")
    side, core = tp // 2, tp % 2
    mate = side * 2 + 1 - core
    across = (1 - side) * 2 + core

    barrier = pltpu.get_barrier_semaphore()

    def greet(offset, carry):
        pl.semaphore_signal(
            barrier, inc=1, device_id={"ctx": peer(me, offset)}, device_id_type=MESH
        )
        return carry

    lax.fori_loop(1, CTX, greet, 0)
    for other in (mate, across):
        pl.semaphore_signal(barrier, inc=1, device_id={"tp": other}, device_id_type=MESH)

    loads = [
        pltpu.make_async_copy(source, target, load_sem.at[slot])
        for slot, (source, target) in enumerate(
            (
                (key_hbm, key),
                (value_hbm, value),
                (filter_hbm, taps),
                (gate_hbm, gate),
                (weight_hbm, weight),
            )
        )
    ]
    for load in loads:
        load.start()
    loads[0].wait()
    loads[1].wait()

    def multiply(row, carry):
        product = key[row].astype(jnp.float32) * value[row].astype(jnp.float32)
        mixed[row] = product.astype(jnp.bfloat16)
        return carry

    lax.fori_loop(0, CTX, multiply, 0, unroll=4)
    for part in range(8):
        spread = jnp.broadcast_to(skip_ref[part : part + 1, :], (128, 128)).T
        for half in range(2):
            rows = mixed[part * 8 : part * 8 + 8, :, :, half * 128 : half * 128 + 128]
            rows = rows.astype(jnp.float32).reshape(128, 128)
            skipped[half, part * 128 : part * 128 + 128, :] = spread * rows
    loads[2].wait()

    pl.semaphore_wait(barrier, CTX + 1)

    def sent_in(chunk, which, target):
        source, landing = ((taps, in_taps), (mixed, in_mixed))[which]
        return pltpu.make_async_remote_copy(
            src_ref=source.at[target, chunk],
            dst_ref=landing.at[chunk, me],
            send_sem=in_send_sem.at[chunk, which],
            recv_sem=in_recv_sem.at[chunk, which],
            device_id={"ctx": target},
            device_id_type=MESH,
        )

    for chunk in range(CHUNKS):

        def push(offset, carry, chunk=chunk):
            target = peer(me, offset)
            sent_in(chunk, 0, target).start()
            sent_in(chunk, 1, target).start()
            return carry

        lax.fori_loop(1, CTX, push, 0)
    for chunk in range(CHUNKS):
        in_taps[chunk, me] = taps[me, chunk]
        in_mixed[chunk, me] = mixed[me, chunk]

    def wait_in(chunk, which, receive):
        source, landing = ((taps, in_taps), (mixed, in_mixed))[which]
        whole = landing.at[chunk, pl.ds(0, CTX - 1)]
        copy = pltpu.make_async_remote_copy(
            src_ref=whole,
            dst_ref=whole,
            send_sem=in_send_sem.at[chunk, which],
            recv_sem=in_recv_sem.at[chunk, which],
            device_id={"ctx": peer(me, 1)},
            device_id_type=MESH,
        )
        if receive:
            copy.wait_recv()
        else:
            copy.wait_send()

    def transform(stage, channel):
        rows = stage.reshape(BASE * GROUP, BASE)[pl.ds(channel, BASE, stride=GROUP), :]
        both = dot(first_ref[...], rows.astype(jnp.bfloat16))
        real, imag = both[:BASE], both[BASE:]
        cos, sin = twist_ref[0], twist_ref[1]
        turned = jnp.concatenate([real * cos - imag * sin, real * sin + imag * cos], 1)
        return dot(turned.astype(jnp.bfloat16), second_ref[...])

    for chunk in range(CHUNKS):
        wait_in(chunk, 0, True)
        wait_in(chunk, 1, True)

        def spread(row, carry, chunk=chunk):
            for landing, stage in ((in_taps, stage_taps), (in_mixed, stage_mixed)):
                block = landing[chunk, row].astype(jnp.float32)
                stage[row, 0] = block[:, :128]
                stage[row, 1] = block[:, 128:]
            return carry

        lax.fori_loop(0, CTX, spread, 0, unroll=8)

        for channel in range(GROUP):
            left = transform(stage_taps, channel)
            right = transform(stage_mixed, channel)
            left_real, left_imag = left[:, :BASE], left[:, BASE:]
            right_real, right_imag = right[:, :BASE], right[:, BASE:]
            product = jnp.concatenate(
                [
                    left_real * right_real - left_imag * right_imag,
                    left_real * right_imag + left_imag * right_real,
                ],
                1,
            )
            back = dot(product.astype(jnp.bfloat16), second_back_ref[...])
            real, imag = back[:, :BASE], back[:, BASE:]
            cos, sin = twist_ref[0], twist_ref[1]
            unturned = jnp.concatenate([real * cos + imag * sin, imag * cos - real * sin], 0)
            conv = dot(first_back_ref[...], unturned.astype(jnp.bfloat16))
            stage_out.reshape(BASE * GROUP, BASE)[pl.ds(channel, BASE, stride=GROUP), :] = conv

        def gather(row, carry, chunk=chunk):
            for half in range(2):
                back_send[half, chunk, row] = stage_out[row, half].astype(jnp.bfloat16)
            return carry

        lax.fori_loop(0, CTX, gather, 0, unroll=8)
        for half in range(2):

            def push_back(offset, carry, half=half, chunk=chunk):
                target = peer(me, offset)
                pltpu.make_async_remote_copy(
                    src_ref=back_send.at[half, chunk, target],
                    dst_ref=back_recv.at[half, me * CHUNKS + chunk],
                    send_sem=back_send_sem.at[half],
                    recv_sem=back_recv_sem.at[half],
                    device_id={"ctx": target},
                    device_id_type=MESH,
                ).start()
                return carry

            lax.fori_loop(1, CTX, push_back, 0)
            back_recv[half, me * CHUNKS + chunk] = back_send[half, chunk, me]

    def wait_back(half):
        whole = back_recv.at[half, pl.ds(0, (CTX - 1) * CHUNKS)]
        return pltpu.make_async_remote_copy(
            src_ref=whole,
            dst_ref=whole,
            send_sem=back_send_sem.at[half],
            recv_sem=back_recv_sem.at[half],
            device_id={"ctx": peer(me, 1)},
            device_id_type=MESH,
        )

    def to_mate(half, slot):
        return pltpu.make_async_remote_copy(
            src_ref=core_send.at[half, slot],
            dst_ref=core_recv.at[half, slot],
            send_sem=core_send_sem.at[half, slot],
            recv_sem=core_recv_sem.at[half, slot],
            device_id={"tp": mate},
            device_id_type=MESH,
        )

    def to_across(half):
        return pltpu.make_async_remote_copy(
            src_ref=y_send.at[half],
            dst_ref=y_recv.at[half],
            send_sem=y_send_sem.at[half],
            recv_sem=y_recv_sem.at[half],
            device_id={"tp": across},
            device_id_type=MESH,
        )

    tile = 256

    def project(half, block, store):
        def step(index, carry):
            start = pl.multiple_of(index * tile, tile)
            rows = weight[pl.ds(pl.multiple_of(block * 1024, 1024) + start, tile), :]
            store(pl.ds(start, tile), dot(rows, gated[half]))
            return carry

        lax.fori_loop(0, 1024 // tile, step, 0)

    loads[3].wait()
    loads[4].wait()
    for half in range(2):
        wait_back(half).wait_recv()
        for part in range(8):
            lanes = slice(half * 128, half * 128 + 128)
            block = slice(part * 16, part * 16 + 16)
            conv = back_recv[half, block].astype(jnp.float32).reshape(128, 128)
            gates = gate[block, :, lanes].astype(jnp.float32).reshape(128, 128)
            rows = slice(part * 128, part * 128 + 128)
            gated[half, rows, :] = (gates * (conv + skipped[half, rows, :])).astype(jnp.bfloat16)

        for slot, owner in enumerate((1 - side, side)):

            def send_rows(rows, value, half=half, slot=slot):
                core_send[half, slot, rows, :] = value.astype(jnp.bfloat16)

            def keep_rows(rows, value, half=half, slot=slot):
                keep[half, slot, rows, :] = value

            project(half, owner * 2 + 1 - core, send_rows)
            to_mate(half, slot).start()
            project(half, owner * 2 + core, keep_rows)
            to_mate(half, slot).wait_recv()
            if slot == 0:
                summed = keep[half, 0] + core_recv[half, 0].astype(jnp.float32)
                y_send[half] = summed.astype(jnp.bfloat16)
                to_across(half).start()

    for half in range(2):
        to_across(half).wait_recv()
        total = (
            keep[half, 1]
            + core_recv[half, 1].astype(jnp.float32)
            + y_recv[half].astype(jnp.float32)
        )
        out_ref[:, half * 128 : half * 128 + 128] = total.astype(jnp.bfloat16)

    for chunk in range(CHUNKS):
        wait_in(chunk, 0, False)
        wait_in(chunk, 1, False)
    for half in range(2):
        wait_back(half).wait_send()
        to_mate(half, 0).wait_send()
        to_mate(half, 1).wait_send()
        to_across(half).wait_send()


def body(gate_branch, key_branch, value_branch, long_filter, skip_gain, out_weight):
    low, full = jnp.bfloat16, jnp.float32
    dma = pltpu.SemaphoreType.DMA
    messages = (CTX, CHUNKS, GROUP, 256)
    anywhere = pl.BlockSpec(memory_space=pl.ANY)
    local = pl.BlockSpec(memory_space=pltpu.VMEM)
    return pl.pallas_call(
        kernel,
        out_shape=jax.ShapeDtypeStruct((1024, 256), low),
        in_specs=[anywhere] * 4 + [local] + [anywhere] + [local] * 5,
        out_specs=local,
        scratch_shapes=[
            pltpu.VMEM((128, 8, 256), low),
            pltpu.VMEM(messages, low),
            pltpu.VMEM(messages, low),
            pltpu.VMEM(messages, low),
            pltpu.VMEM((4096, 1024), low),
            pltpu.VMEM(messages, low),
            pltpu.VMEM((2, 1024, 128), full),
            pltpu.VMEM((CHUNKS, CTX, GROUP, 256), low),
            pltpu.VMEM((CHUNKS, CTX, GROUP, 256), low),
            pltpu.VMEM((CTX, 2, GROUP, 128), full),
            pltpu.VMEM((CTX, 2, GROUP, 128), full),
            pltpu.VMEM((CTX, 2, GROUP, 128), full),
            pltpu.VMEM((2, CHUNKS, CTX, GROUP, 128), low),
            pltpu.VMEM((2, CTX * CHUNKS, GROUP, 128), low),
            pltpu.VMEM((2, 1024, 128), low),
            pltpu.VMEM((2, 2, 1024, 128), low),
            pltpu.VMEM((2, 2, 1024, 128), low),
            pltpu.VMEM((2, 2, 1024, 128), full),
            pltpu.VMEM((2, 1024, 128), low),
            pltpu.VMEM((2, 1024, 128), low),
            dma((5,)),
            dma((CHUNKS, 2)),
            dma((CHUNKS, 2)),
            dma((2,)),
            dma((2,)),
            dma((2, 2)),
            dma((2, 2)),
            dma((2,)),
            dma((2,)),
        ],
        compiler_params=pltpu.CompilerParams(
            collective_id=0, has_side_effects=True, vmem_limit_bytes=60 * 1024 * 1024
        ),
    )(
        gate_branch.reshape(128, 8, 256),
        key_branch.reshape(messages),
        value_branch.reshape(messages),
        long_filter.reshape(messages),
        skip_gain.reshape(8, 128),
        out_weight,
        *tables(),
    )


def solution(mesh):
    placed = (
        P("tp", "ctx"),
        P("tp", "ctx"),
        P("tp", "ctx"),
        P("tp", "ctx"),
        P("tp"),
        P(None, "tp"),
    )
    return jax.shard_map(
        body, mesh=mesh, in_specs=placed, out_specs=P("tp", "ctx"), check_vma=False
    )
```

time: 150 us -> 75.5 us (0.50); the launches traced: 147 us -> 75.3 us
  Pallas kernels: 0 us -> 73.5 us
  blocking collectives: 54.6 us -> 0 us
  matrix products: 41.4 us -> 0 us
  waiting for transfers between devices: 22.7 us -> 0 us
  starting transfers between devices: 22.2 us -> 0 us
  other arithmetic: 3.27 us -> 0 us
    pallas_call x0 -> x1, Pallas kernels: none -> 73.5 us  [body(): pl.pallas_call(kernel, out_shape=jax.ShapeDtypeStruct((1024, 256), low),...]
    all_to_all x2 -> x0, blocking collectives: 54.6 us -> none  [the longest x1 31.4 us: summed_on_arrival(): tiles = lax.all_to_all(split_up(shard, dim, size), axis, 0, 0, tiled=True)]
    dot_general x19 -> x0, matrix products: 41.4 us -> none  [the longest x12 32 us: right_mul(): return jnp.einsum('kcb,bd->kcd', left, table, precision=triple)]
    all_to_all x2 -> x0, waiting for transfers between devices: 22.7 us -> none  [the longest x1 15.3 us: body(): lax.all_to_all(long_filter, 'ctx', split_axis=0, concat_axis=1, tiled=True)]
    all_to_all x2 -> x0, starting transfers between devices: 22.2 us -> none  [the longest x1 15.2 us: body(): lax.all_to_all(long_filter, 'ctx', split_axis=0, concat_axis=1, tiled=True)]
    convert_element_type x2 -> x0, other arithmetic: 2.31 us -> none  [the longest x1 1.39 us: body(): gated = gated.astype(jnp.bfloat16)]
    unnamed x24 -> x1, local copies, waits for them, and re-layouts: 0.06 us -> 1.87 us
  transfers between devices with their start and end apart: 2 -> 0, of which waited for: 2 -> 0; matrix products, arithmetic and copies ran while one was open for 8% -> 0% of each run, Pallas kernels for 0% -> 0%
where the time goes in v1:
time: 75.5 us; the launch traced here: 75.3 us
  Pallas kernels  73.5 us (97%)
  local copies, waits for them, and re-layouts  1.87 us (2%)
    pallas_call x1, Pallas kernels, body(): pl.pallas_call(kernel, out_shape=jax.ShapeDtypeStruct((1024, 256), low),...  73.5 us
    unnamed x1, local copies, waits for them, and re-layouts  1.87 us

profile of v1, /device:TPU:1, one launch (start us, length us, event | category | flops | bytes accessed | tf_op | source)
XLA Modules:
  0.0 75.3 jit_solution(12029804940576322523)
XLA Ops:
  0.0 73.5 %shard_map.109 = bf16[1024,256]{1,0:T(8,128)(2,1)} custom-call(bf16[128,8,256]{2,1,0:T(8,128)(2,1)} %bitcast.5, bf16[64,2,8,256]{3,2,1,0:T(8,128)(2,1)} %bitcast.6, bf16[64,2,8,256]{3,2,1,0:T(8,128)(2,1)} %bitcast.7, bf16[64,2,8,256]{3,2,1,0:T(8,128)(2,1)} %bitcast.8, f32[8,128]{1,0:T(8,128)} %bitcast.9, bf16[4096,1024]{1,0:T(8,128)(2,1)} %weight_hbm.1, ...), custom_call_target="tpu_custom_call" | custom-call | tf_op jit(solution)/shard_map/pallas_call | solution.py:340
  73.5 1.9 %copy.13 = bf16[1024,256]{1,0:T(8,128)(2,1)} copy(bf16[1024,256]{1,0:T(8,128)(2,1)} %shard_map.109) | data formatting | bytes 1048576

commit v2 on v1

v2 whole, which is shorter than its diff:
```python
import functools

import jax
import jax.numpy as jnp
import numpy as np
from jax import lax
from jax.experimental import pallas as pl
from jax.experimental.pallas import tpu as pltpu
from jax.sharding import PartitionSpec as P

MESH = pl.DeviceIdType.MESH
CTX = 64
TP = 4
BASE = 128
CHUNKS = 2
GROUP = 8
PIECE = 256
PIECES = 1024 // PIECE


def tables():
    index = np.arange(BASE)
    first = np.exp(2j * np.pi * np.outer(index + 0.25, index) / BASE)
    twist = np.exp(2j * np.pi * np.outer(index + 0.25, index) / BASE**2)
    second = np.exp(2j * np.pi * np.outer(index, index) / BASE)
    back = first.T / BASE**2
    low = lambda table: jnp.asarray(table, jnp.bfloat16)
    return (
        low(np.concatenate([first.real, first.imag], 0)),
        low(np.block([[second.real, second.imag], [-second.imag, second.real]])),
        low(np.block([[second.real, -second.imag], [second.imag, second.real]])),
        low(np.concatenate([back.real, back.imag], 1)),
        jnp.asarray(np.stack([twist.real, twist.imag]), jnp.float32),
    )


def every_peer(me, act):
    high, z, x = me // 32 * 32, (me // 4) % 8, me % 4
    near = [(x + step) % 4 for step in range(4)]
    far = [(z + step) % 8 * 4 for step in range(8)]
    halves = (high, 32 - high)
    for dz, dy, dx in ORDER:
        act(halves[dy] + far[dz] + near[dx])


ORDER = [(4, 1, 2), (3, 1, 2), (4, 1, 1), (4, 1, 3), (5, 1, 2), (2, 1, 2), (3, 1, 1), (3, 1, 3), (4, 0, 2), (4, 1, 0), (5, 1, 1), (5, 1, 3), (6, 1, 2), (1, 1, 2), (2, 1, 1), (2, 1, 3), (3, 0, 2), (3, 1, 0), (4, 0, 1), (4, 0, 3), (5, 0, 2), (5, 1, 0), (6, 1, 1), (6, 1, 3), (7, 1, 2), (0, 1, 2), (1, 1, 1), (1, 1, 3), (2, 0, 2), (2, 1, 0), (3, 0, 1), (3, 0, 3), (4, 0, 0), (5, 0, 1), (5, 0, 3), (6, 0, 2), (6, 1, 0), (7, 1, 1), (7, 1, 3), (0, 1, 1), (0, 1, 3), (1, 0, 2), (1, 1, 0), (2, 0, 1), (2, 0, 3), (3, 0, 0), (5, 0, 0), (6, 0, 1), (6, 0, 3), (7, 0, 2), (7, 1, 0), (0, 0, 2), (0, 1, 0), (1, 0, 1), (1, 0, 3), (2, 0, 0), (6, 0, 0), (7, 0, 1), (7, 0, 3), (0, 0, 1), (0, 0, 3), (1, 0, 0), (7, 0, 0)]


def dot(left, right):
    return jnp.dot(left, right, preferred_element_type=jnp.float32)


def kernel(
    gate_hbm,
    key_hbm,
    value_hbm,
    filter_hbm,
    skip_ref,
    weight_hbm,
    first_ref,
    second_ref,
    second_back_ref,
    first_back_ref,
    twist_ref,
    own_hbm,
    other_hbm,
    gate,
    key,
    value,
    taps,
    weight,
    mixed,
    skipped,
    in_mixed,
    in_taps,
    stage_mixed,
    stage_taps,
    stage_out,
    spectra_taps,
    back_send,
    back_recv,
    gated,
    core_send,
    core_recv,
    keep,
    y_send,
    own,
    load_sem,
    in_send_sem,
    in_recv_sem,
    back_send_sem,
    back_recv_sem,
    core_send_sem,
    core_recv_sem,
    y_send_sem,
    y_recv_sem,
    own_sem,
):
    me, tp = lax.axis_index("ctx"), lax.axis_index("tp")
    side, core = tp // 2, tp % 2
    mate = side * 2 + 1 - core
    across = (1 - side) * 2 + core

    barrier = pltpu.get_barrier_semaphore()

    loads = [
        pltpu.make_async_copy(source, target, load_sem.at[slot])
        for slot, (source, target) in enumerate(
            (
                (filter_hbm, taps),
                (key_hbm, key),
                (value_hbm, value),
                (gate_hbm, gate),
                (weight_hbm, weight),
            )
        )
    ]
    loads[0].start()
    every_peer(
        me,
        lambda other: pl.semaphore_signal(
            barrier, inc=1, device_id={"ctx": other}, device_id_type=MESH
        ),
    )
    for other in (mate, across):
        pl.semaphore_signal(barrier, inc=1, device_id={"tp": other}, device_id_type=MESH)

    for load in loads[1:]:
        load.start()

    def multiply(chunk):
        def step(row, carry):
            product = key[row, chunk].astype(jnp.float32) * value[row, chunk].astype(jnp.float32)
            mixed[row, chunk] = product.astype(jnp.bfloat16)
            return carry

        lax.fori_loop(0, CTX, step, 0, unroll=8)

    def skip():
        for part in range(8):
            spread = jnp.broadcast_to(skip_ref[part : part + 1, :], (128, 128)).T
            for half in range(2):
                rows = mixed[part * 8 : part * 8 + 8, :, :, half * 128 : half * 128 + 128]
                rows = rows.astype(jnp.float32).reshape(128, 128)
                skipped[half, part * 128 : part * 128 + 128, :] = spread * rows

    def sent_in(chunk, which, target):
        source, landing = ((taps, in_taps), (mixed, in_mixed))[which]
        return pltpu.make_async_remote_copy(
            src_ref=source.at[target, chunk],
            dst_ref=landing.at[chunk, me],
            send_sem=in_send_sem.at[chunk, which],
            recv_sem=in_recv_sem.at[chunk, which],
            device_id={"ctx": target},
            device_id_type=MESH,
        )

    def push_in(chunk, which):
        every_peer(me, lambda other: sent_in(chunk, which, other).start())
        source, landing = ((taps, in_taps), (mixed, in_mixed))[which]
        landing[chunk, me] = source[me, chunk]

    def wait_in(chunk, which, receive):
        source, landing = ((taps, in_taps), (mixed, in_mixed))[which]
        whole = landing.at[chunk, pl.ds(0, CTX - 1)]
        copy = pltpu.make_async_remote_copy(
            src_ref=whole,
            dst_ref=whole,
            send_sem=in_send_sem.at[chunk, which],
            recv_sem=in_recv_sem.at[chunk, which],
            device_id={"ctx": (me + 1) % CTX},
            device_id_type=MESH,
        )
        if receive:
            copy.wait_recv()
        else:
            copy.wait_send()

    cos, sin = twist_ref[0], twist_ref[1]

    def spread(chunk, landing, stage):
        def step(row, carry):
            block = landing[chunk, row].astype(jnp.float32)
            stage[row, 0] = block[:, :128]
            stage[row, 1] = block[:, 128:]
            return carry

        lax.fori_loop(0, CTX, step, 0, unroll=8)

    def transform(stage, pair):
        flat = stage.reshape(BASE * GROUP, BASE)
        rows = [flat[pl.ds(2 * pair + one, BASE, stride=GROUP), :] for one in range(2)]
        both = dot(first_ref[...], jnp.concatenate(rows, 1).astype(jnp.bfloat16))
        spectra = []
        for one in range(2):
            real = both[:BASE, one * BASE : one * BASE + BASE]
            imag = both[BASE:, one * BASE : one * BASE + BASE]
            turned = jnp.concatenate([real * cos - imag * sin, real * sin + imag * cos], 1)
            spectra.append(dot(turned.astype(jnp.bfloat16), second_ref[...]))
        return spectra

    def transform_taps(chunk):
        spread(chunk, in_taps, stage_taps)
        for pair in range(GROUP // 2):
            for one, spectrum in enumerate(transform(stage_taps, pair)):
                spectra_taps[chunk, 2 * pair + one] = spectrum

    def convolve(chunk):
        spread(chunk, in_mixed, stage_mixed)
        for pair in range(GROUP // 2):
            halves = []
            for one, right in enumerate(transform(stage_mixed, pair)):
                left = spectra_taps[chunk, 2 * pair + one]
                left_real, left_imag = left[:, :BASE], left[:, BASE:]
                right_real, right_imag = right[:, :BASE], right[:, BASE:]
                product = jnp.concatenate(
                    [
                        left_real * right_real - left_imag * right_imag,
                        left_real * right_imag + left_imag * right_real,
                    ],
                    1,
                )
                back = dot(product.astype(jnp.bfloat16), second_back_ref[...])
                real, imag = back[:, :BASE], back[:, BASE:]
                halves.append(
                    jnp.concatenate([real * cos + imag * sin, imag * cos - real * sin], 0)
                )
            unturned = jnp.concatenate(halves, 1).astype(jnp.bfloat16)
            conv = dot(first_back_ref[...], unturned)
            flat = stage_out.reshape(BASE * GROUP, BASE)
            for one in range(2):
                flat[pl.ds(2 * pair + one, BASE, stride=GROUP), :] = conv[
                    :, one * BASE : one * BASE + BASE
                ]

        def gather(row, carry):
            for half in range(2):
                back_send[half, chunk, row] = stage_out[row, half].astype(jnp.bfloat16)
            return carry

        lax.fori_loop(0, CTX, gather, 0, unroll=8)
        for half in range(2):
            back_recv[half, me * CHUNKS + chunk] = back_send[half, chunk, me]

    def push_back(half, chunk):
        def send(target):
            pltpu.make_async_remote_copy(
                src_ref=back_send.at[half, chunk, target],
                dst_ref=back_recv.at[half, me * CHUNKS + chunk],
                send_sem=back_send_sem.at[half],
                recv_sem=back_recv_sem.at[half],
                device_id={"ctx": target},
                device_id_type=MESH,
            ).start()

        every_peer(me, send)

    loads[0].wait()
    pl.semaphore_wait(barrier, CTX + 1)
    push_in(0, 0)
    push_in(1, 0)
    loads[1].wait()
    loads[2].wait()
    multiply(0)
    push_in(0, 1)
    multiply(1)
    push_in(1, 1)
    skip()
    wait_in(0, 0, True)
    transform_taps(0)
    wait_in(1, 0, True)
    transform_taps(1)
    wait_in(0, 1, True)
    convolve(0)
    push_back(0, 0)
    wait_in(1, 1, True)
    convolve(1)
    push_back(0, 1)
    push_back(1, 0)
    push_back(1, 1)

    def wait_back(half):
        whole = back_recv.at[half, pl.ds(0, (CTX - 1) * CHUNKS)]
        return pltpu.make_async_remote_copy(
            src_ref=whole,
            dst_ref=whole,
            send_sem=back_send_sem.at[half],
            recv_sem=back_recv_sem.at[half],
            device_id={"ctx": (me + 1) % CTX},
            device_id_type=MESH,
        )

    def to_mate(half, slot, piece):
        rows = pl.ds(pl.multiple_of(piece * PIECE, PIECE), PIECE)
        return pltpu.make_async_remote_copy(
            src_ref=core_send.at[half, slot, rows],
            dst_ref=core_recv.at[half, slot, rows],
            send_sem=core_send_sem.at[half, slot, piece],
            recv_sem=core_recv_sem.at[half, slot, piece],
            device_id={"tp": mate},
            device_id_type=MESH,
        )

    def to_across(half, rows):
        return pltpu.make_async_remote_copy(
            src_ref=y_send.at[half, rows],
            dst_ref=other_hbm.at[rows, pl.ds(half * 128, 128)],
            send_sem=y_send_sem.at[half],
            recv_sem=y_recv_sem.at[half],
            device_id={"tp": across},
            device_id_type=MESH,
        )

    def own_out(half):
        return pltpu.make_async_copy(
            own.at[half], own_hbm.at[:, pl.ds(half * 128, 128)], own_sem.at[half]
        )

    loads[3].wait()
    loads[4].wait()
    for half in range(2):
        wait_back(half).wait_recv()
        for part in range(8):
            lanes = slice(half * 128, half * 128 + 128)
            block = slice(part * 16, part * 16 + 16)
            conv = back_recv[half, block].astype(jnp.float32).reshape(128, 128)
            gates = gate[block, :, lanes].astype(jnp.float32).reshape(128, 128)
            rows = slice(part * 128, part * 128 + 128)
            gated[half, rows, :] = (gates * (conv + skipped[half, rows, :])).astype(jnp.bfloat16)

        def project(step, half=half):
            slot, piece = step // PIECES, step % PIECES
            owner = (side + 1 - slot) % 2
            rows = pl.ds(pl.multiple_of(piece * PIECE, PIECE), PIECE)

            def part(block):
                start = pl.multiple_of(block * 1024 + piece * PIECE, PIECE)
                return dot(weight[pl.ds(start, PIECE), :], gated[half])

            core_send[half, slot, rows, :] = part(owner * 2 + 1 - core).astype(jnp.bfloat16)
            to_mate(half, slot, piece).start()
            keep[half, slot, rows, :] = part(owner * 2 + core)

        def combine(step, half=half):
            slot, piece = step // PIECES, step % PIECES
            rows = pl.ds(pl.multiple_of(piece * PIECE, PIECE), PIECE)
            to_mate(half, slot, piece).wait_recv()
            summed = keep[half, slot, rows, :] + core_recv[half, slot, rows, :].astype(jnp.float32)

            @pl.when(slot == 0)
            def _():
                y_send[half, rows, :] = summed.astype(jnp.bfloat16)
                to_across(half, rows).start()

            @pl.when(slot == 1)
            def _():
                own[half, rows, :] = summed.astype(jnp.bfloat16)

        def advance(step, carry):
            project(step)

            @pl.when(step > 0)
            def _():
                combine(step - 1)

            return carry

        lax.fori_loop(0, 2 * PIECES, advance, 0)
        combine(2 * PIECES - 1)
        own_out(half).start()

    for chunk in range(CHUNKS):
        wait_in(chunk, 0, False)
        wait_in(chunk, 1, False)
    for half in range(2):
        wait_back(half).wait_send()
        for slot in range(2):
            for piece in range(PIECES):
                to_mate(half, slot, piece).wait_send()
        own_out(half).wait()
        to_across(half, pl.ds(0, 1024)).wait_send()
        to_across(half, pl.ds(0, 1024)).wait_recv()


def body(gate_branch, key_branch, value_branch, long_filter, skip_gain, out_weight):
    low, full = jnp.bfloat16, jnp.float32
    dma = pltpu.SemaphoreType.DMA
    messages = (CTX, CHUNKS, GROUP, 256)
    anywhere = pl.BlockSpec(memory_space=pl.ANY)
    local = pl.BlockSpec(memory_space=pltpu.VMEM)
    own, other = pl.pallas_call(
        kernel,
        out_shape=[jax.ShapeDtypeStruct((1024, 256), low)] * 2,
        in_specs=[anywhere] * 4 + [local] + [anywhere] + [local] * 5,
        out_specs=[anywhere] * 2,
        scratch_shapes=[
            pltpu.VMEM((128, 8, 256), low),
            pltpu.VMEM(messages, low),
            pltpu.VMEM(messages, low),
            pltpu.VMEM(messages, low),
            pltpu.VMEM((4096, 1024), low),
            pltpu.VMEM(messages, low),
            pltpu.VMEM((2, 1024, 128), full),
            pltpu.VMEM((CHUNKS, CTX, GROUP, 256), low),
            pltpu.VMEM((CHUNKS, CTX, GROUP, 256), low),
            pltpu.VMEM((CTX, 2, GROUP, 128), full),
            pltpu.VMEM((CTX, 2, GROUP, 128), full),
            pltpu.VMEM((CTX, 2, GROUP, 128), full),
            pltpu.VMEM((CHUNKS, GROUP, BASE, 2 * BASE), full),
            pltpu.VMEM((2, CHUNKS, CTX, GROUP, 128), low),
            pltpu.VMEM((2, CTX * CHUNKS, GROUP, 128), low),
            pltpu.VMEM((2, 1024, 128), low),
            pltpu.VMEM((2, 2, 1024, 128), low),
            pltpu.VMEM((2, 2, 1024, 128), low),
            pltpu.VMEM((2, 2, 1024, 128), full),
            pltpu.VMEM((2, 1024, 128), low),
            pltpu.VMEM((2, 1024, 128), low),
            dma((5,)),
            dma((CHUNKS, 2)),
            dma((CHUNKS, 2)),
            dma((2,)),
            dma((2,)),
            dma((2, 2, PIECES)),
            dma((2, 2, PIECES)),
            dma((2,)),
            dma((2,)),
            dma((2,)),
        ],
        compiler_params=pltpu.CompilerParams(
            collective_id=0, has_side_effects=True, vmem_limit_bytes=60 * 1024 * 1024
        ),
    )(
        gate_branch.reshape(128, 8, 256),
        key_branch.reshape(messages),
        value_branch.reshape(messages),
        long_filter.reshape(messages),
        skip_gain.reshape(8, 128),
        out_weight,
        *tables(),
    )
    return (own.astype(full) + other.astype(full)).astype(low)


def solution(mesh):
    placed = (
        P("tp", "ctx"),
        P("tp", "ctx"),
        P("tp", "ctx"),
        P("tp", "ctx"),
        P("tp"),
        P(None, "tp"),
    )
    return jax.shard_map(
        body, mesh=mesh, in_specs=placed, out_specs=P("tp", "ctx"), check_vma=False
    )
```

time: 75.5 us -> 66.8 us (0.88)
  Pallas kernels: 73.5 us -> 64.5 us
  other arithmetic: 0 us -> 2.12 us
  local copies, waits for them, and re-layouts: 1.87 us -> 0 us
    pallas_call x1, Pallas kernels: 73.5 us -> 64.5 us  [body(): pl.pallas_call(kernel, out_shape=[jax.ShapeDtypeStruct((1024, 256), low)]...]
    convert_element_type x0 -> x1, other arithmetic: none -> 2.12 us  [body(): return (own.astype(full) + other.astype(full)).astype(low)]
    unnamed x1 -> x0, local copies, waits for them, and re-layouts: 1.87 us -> none
where the time goes in v2:
time: 66.8 us; the launch traced here: 66.7 us
  Pallas kernels  64.5 us (97%)
  other arithmetic  2.12 us (3%)
    pallas_call x1, Pallas kernels, body(): pl.pallas_call(kernel, out_shape=[jax.ShapeDtypeStruct((1024, 256), low)]...  64.5 us
    convert_element_type x1, other arithmetic, body(): return (own.astype(full) + other.astype(full)).astype(low)  2.12 us

profile of v2, /device:TPU:1, one launch (start us, length us, event | category | flops | bytes accessed | tf_op | source)
XLA Modules:
  0.0 66.7 jit_solution(6723599295280869502)
XLA Ops:
  0.0 64.5 %shard_map.109 = (bf16[1024,256]{1,0:T(8,128)(2,1)}, bf16[1024,256]{1,0:T(8,128)(2,1)}) custom-call(bf16[128,8,256]{2,1,0:T(8,128)(2,1)} %bitcast.5, bf16[64,2,8,256]{3,2,1,0:T(8,128)(2,1)} %bitcast.6, bf16[64,2,8,256]{3,2,1,0:T(8,128)(2,1)} %bitcast.7, bf16[64,2,8,256]{3,2,1,0:T(8,128)(2,1)} %bitcast.8, f32[8,128]{1,0:T(8,128)} %bitcast.9, ...), custom_call_target="tpu_custom_call" | custom-call | tf_op jit(solution)/shard_map/pallas_call | solution.py:391
  64.5 2.1 %add_convert_fusion = bf16[1024,256]{1,0:T(8,128)(2,1)} fusion(bf16[1024,256]{1,0:T(8,128)(2,1)} %get-tuple-element.8, bf16[1024,256]{1,0:T(8,128)(2,1)} %get-tuple-element.7), kind=kLoop, calls=%fused_computation | loop fusion | flops 1048576 | bytes 1572864 | tf_op jit(solution)/shard_map/convert_element_type | solution.py:441

commit v3 on v2

--- a/solution.py
+++ b/solution.py
@@ -14,6 +14,7 @@
 BASE = 128
 CHUNKS = 2
 GROUP = 8
+SPAN = 8
 PIECE = 256
 PIECES = 1024 // PIECE
 
@@ -55,13 +56,13 @@
     key_hbm,
     value_hbm,
     filter_hbm,
-    skip_ref,
+    skip_hbm,
     weight_hbm,
-    first_ref,
-    second_ref,
-    second_back_ref,
-    first_back_ref,
-    twist_ref,
+    first_hbm,
+    second_hbm,
+    second_back_hbm,
+    first_back_hbm,
+    twist_hbm,
     own_hbm,
     other_hbm,
     gate,
@@ -85,6 +86,12 @@
     keep,
     y_send,
     own,
+    skip_ref,
+    first_ref,
+    second_ref,
+    second_back_ref,
+    first_back_ref,
+    twist_ref,
     load_sem,
     in_send_sem,
     in_recv_sem,
@@ -110,6 +117,12 @@
                 (filter_hbm, taps),
                 (key_hbm, key),
                 (value_hbm, value),
+                (skip_hbm, skip_ref),
+                (first_hbm, first_ref),
+                (second_hbm, second_ref),
+                (second_back_hbm, second_back_ref),
+                (first_back_hbm, first_back_ref),
+                (twist_hbm, twist_ref),
                 (gate_hbm, gate),
                 (weight_hbm, weight),
             )
@@ -176,8 +189,6 @@
         else:
             copy.wait_send()
 
-    cos, sin = twist_ref[0], twist_ref[1]
-
     def spread(chunk, landing, stage):
         def step(row, carry):
             block = landing[chunk, row].astype(jnp.float32)
@@ -187,49 +198,53 @@
 
         lax.fori_loop(0, CTX, step, 0, unroll=8)
 
-    def transform(stage, pair):
+    def transform(stage, first_channel):
+        cos, sin = twist_ref[0], twist_ref[1]
         flat = stage.reshape(BASE * GROUP, BASE)
-        rows = [flat[pl.ds(2 * pair + one, BASE, stride=GROUP), :] for one in range(2)]
-        both = dot(first_ref[...], jnp.concatenate(rows, 1).astype(jnp.bfloat16))
-        spectra = []
-        for one in range(2):
+        rows = [
+            flat[pl.ds(first_channel + one, BASE, stride=GROUP), :].astype(jnp.bfloat16)
+            for one in range(SPAN)
+        ]
+        both = dot(first_ref[...], jnp.concatenate(rows, 1))
+        turned = []
+        for one in range(SPAN):
             real = both[:BASE, one * BASE : one * BASE + BASE]
             imag = both[BASE:, one * BASE : one * BASE + BASE]
-            turned = jnp.concatenate([real * cos - imag * sin, real * sin + imag * cos], 1)
-            spectra.append(dot(turned.astype(jnp.bfloat16), second_ref[...]))
-        return spectra
+            pieces = [real * cos - imag * sin, real * sin + imag * cos]
+            turned.append(jnp.concatenate([piece.astype(jnp.bfloat16) for piece in pieces], 1))
+        return dot(jnp.concatenate(turned, 0), second_ref[...])
 
     def transform_taps(chunk):
         spread(chunk, in_taps, stage_taps)
-        for pair in range(GROUP // 2):
-            for one, spectrum in enumerate(transform(stage_taps, pair)):
-                spectra_taps[chunk, 2 * pair + one] = spectrum
+        for start in range(0, GROUP, SPAN):
+            spectra_taps[chunk, start * BASE : (start + SPAN) * BASE, :] = transform(
+                stage_taps, start
+            )
 
     def convolve(chunk):
+        cos, sin = twist_ref[0], twist_ref[1]
         spread(chunk, in_mixed, stage_mixed)
-        for pair in range(GROUP // 2):
-            halves = []
-            for one, right in enumerate(transform(stage_mixed, pair)):
-                left = spectra_taps[chunk, 2 * pair + one]
-                left_real, left_imag = left[:, :BASE], left[:, BASE:]
-                right_real, right_imag = right[:, :BASE], right[:, BASE:]
-                product = jnp.concatenate(
-                    [
-                        left_real * right_real - left_imag * right_imag,
-                        left_real * right_imag + left_imag * right_real,
-                    ],
-                    1,
+        flat = stage_out.reshape(BASE * GROUP, BASE)
+        for start in range(0, GROUP, SPAN):
+            right = transform(stage_mixed, start)
+            left = spectra_taps[chunk, start * BASE : (start + SPAN) * BASE, :]
+            left_real, left_imag = left[:, :BASE], left[:, BASE:]
+            right_real, right_imag = right[:, :BASE], right[:, BASE:]
+            real = left_real * right_real - left_imag * right_imag
+            imag = left_real * right_imag + left_imag * right_real
+            product = jnp.concatenate([real.astype(jnp.bfloat16), imag.astype(jnp.bfloat16)], 1)
+            back = dot(product, second_back_ref[...])
+            unturned = []
+            for one in range(SPAN):
+                real = back[one * BASE : one * BASE + BASE, :BASE]
+                imag = back[one * BASE : one * BASE + BASE, BASE:]
+                pieces = [real * cos + imag * sin, imag * cos - real * sin]
+                unturned.append(
+                    jnp.concatenate([piece.astype(jnp.bfloat16) for piece in pieces], 0)
                 )
-                back = dot(product.astype(jnp.bfloat16), second_back_ref[...])
-                real, imag = back[:, :BASE], back[:, BASE:]
-                halves.append(
-                    jnp.concatenate([real * cos + imag * sin, imag * cos - real * sin], 0)
-                )
-            unturned = jnp.concatenate(halves, 1).astype(jnp.bfloat16)
-            conv = dot(first_back_ref[...], unturned)
-            flat = stage_out.reshape(BASE * GROUP, BASE)
-            for one in range(2):
-                flat[pl.ds(2 * pair + one, BASE, stride=GROUP), :] = conv[
+            conv = dot(first_back_ref[...], jnp.concatenate(unturned, 1))
+            for one in range(SPAN):
+                flat[pl.ds(start + one, BASE, stride=GROUP), :] = conv[
                     :, one * BASE : one * BASE + BASE
                 ]
 
@@ -265,6 +280,8 @@
     push_in(0, 1)
     multiply(1)
     push_in(1, 1)
+    for load in loads[3:9]:
+        load.wait()
     skip()
     wait_in(0, 0, True)
     transform_taps(0)
@@ -277,7 +294,11 @@
     convolve(1)
     push_back(0, 1)
     push_back(1, 0)
-    push_back(1, 1)
+
+    @pl.when(core == 0)
+    def _():
+        push_back(1, 1)
+
 
     def wait_back(half):
         whole = back_recv.at[half, pl.ds(0, (CTX - 1) * CHUNKS)]
@@ -316,10 +337,9 @@
             own.at[half], own_hbm.at[:, pl.ds(half * 128, 128)], own_sem.at[half]
         )
 
-    loads[3].wait()
-    loads[4].wait()
-    for half in range(2):
-        wait_back(half).wait_recv()
+    loads[9].wait()
+    loads[10].wait()
+    def gating(half):
         for part in range(8):
             lanes = slice(half * 128, half * 128 + 128)
             block = slice(part * 16, part * 16 + 16)
@@ -328,9 +348,10 @@
             rows = slice(part * 128, part * 128 + 128)
             gated[half, rows, :] = (gates * (conv + skipped[half, rows, :])).astype(jnp.bfloat16)
 
-        def project(step, half=half):
-            slot, piece = step // PIECES, step % PIECES
-            owner = (side + 1 - slot) % 2
+    def sums(half, slot):
+        owner = (side + 1 - slot) % 2
+
+        def project(piece):
             rows = pl.ds(pl.multiple_of(piece * PIECE, PIECE), PIECE)
 
             def part(block):
@@ -341,33 +362,43 @@
             to_mate(half, slot, piece).start()
             keep[half, slot, rows, :] = part(owner * 2 + core)
 
-        def combine(step, half=half):
-            slot, piece = step // PIECES, step % PIECES
+        def combine(piece):
             rows = pl.ds(pl.multiple_of(piece * PIECE, PIECE), PIECE)
             to_mate(half, slot, piece).wait_recv()
             summed = keep[half, slot, rows, :] + core_recv[half, slot, rows, :].astype(jnp.float32)
-
-            @pl.when(slot == 0)
-            def _():
+            if slot == 0:
                 y_send[half, rows, :] = summed.astype(jnp.bfloat16)
                 to_across(half, rows).start()
-
-            @pl.when(slot == 1)
+            else:
+                own[half, rows, :] = summed.astype(jnp.bfloat16)
+
+        def advance(piece, carry):
+            project(piece)
+
+            @pl.when(piece > 0)
             def _():
-                own[half, rows, :] = summed.astype(jnp.bfloat16)
-
-        def advance(step, carry):
-            project(step)
-
-            @pl.when(step > 0)
-            def _():
-                combine(step - 1)
+                combine(piece - 1)
 
             return carry
 
-        lax.fori_loop(0, 2 * PIECES, advance, 0)
-        combine(2 * PIECES - 1)
-        own_out(half).start()
+        lax.fori_loop(0, PIECES, advance, 0)
+        return lambda: combine(PIECES - 1)
+
+    wait_back(0).wait_recv()
+    gating(0)
+
+    @pl.when(core == 1)
+    def _():
+        push_back(1, 1)
+
+    sums(0, 0)()
+    wait_back(1).wait_recv()
+    gating(1)
+    sums(1, 0)()
+    sums(0, 1)()
+    own_out(0).start()
+    sums(1, 1)()
+    own_out(1).start()
 
     for chunk in range(CHUNKS):
         wait_in(chunk, 0, False)
@@ -387,11 +418,10 @@
     dma = pltpu.SemaphoreType.DMA
     messages = (CTX, CHUNKS, GROUP, 256)
     anywhere = pl.BlockSpec(memory_space=pl.ANY)
-    local = pl.BlockSpec(memory_space=pltpu.VMEM)
     own, other = pl.pallas_call(
         kernel,
         out_shape=[jax.ShapeDtypeStruct((1024, 256), low)] * 2,
-        in_specs=[anywhere] * 4 + [local] + [anywhere] + [local] * 5,
+        in_specs=[anywhere] * 11,
         out_specs=[anywhere] * 2,
         scratch_shapes=[
             pltpu.VMEM((128, 8, 256), low),
@@ -406,7 +436,7 @@
             pltpu.VMEM((CTX, 2, GROUP, 128), full),
             pltpu.VMEM((CTX, 2, GROUP, 128), full),
             pltpu.VMEM((CTX, 2, GROUP, 128), full),
-            pltpu.VMEM((CHUNKS, GROUP, BASE, 2 * BASE), full),
+            pltpu.VMEM((CHUNKS, GROUP * BASE, 2 * BASE), full),
             pltpu.VMEM((2, CHUNKS, CTX, GROUP, 128), low),
             pltpu.VMEM((2, CTX * CHUNKS, GROUP, 128), low),
             pltpu.VMEM((2, 1024, 128), low),
@@ -415,7 +445,13 @@
             pltpu.VMEM((2, 2, 1024, 128), full),
             pltpu.VMEM((2, 1024, 128), low),
             pltpu.VMEM((2, 1024, 128), low),
-            dma((5,)),
+            pltpu.VMEM((8, 128), full),
+            pltpu.VMEM((2 * BASE, BASE), low),
+            pltpu.VMEM((2 * BASE, 2 * BASE), low),
+            pltpu.VMEM((2 * BASE, 2 * BASE), low),
+            pltpu.VMEM((BASE, 2 * BASE), low),
+            pltpu.VMEM((2, BASE, BASE), full),
+            dma((11,)),
             dma((CHUNKS, 2)),
             dma((CHUNKS, 2)),
             dma((2,)),

time: 66.8 us -> 64.2 us (0.961)
  Pallas kernels: 64.5 us -> 61.9 us
    pallas_call x1, Pallas kernels: 64.5 us -> 61.9 us  [body(): pl.pallas_call(kernel, out_shape=[jax.ShapeDtypeStruct((1024, 256), low)]...]
where the time goes in v3:
time: 64.2 us; the launch traced here: 64.1 us
  Pallas kernels  61.9 us (96%)
  other arithmetic  2.12 us (3%)
    pallas_call x1, Pallas kernels, body(): pl.pallas_call(kernel, out_shape=[jax.ShapeDtypeStruct((1024, 256), low)]...  61.9 us
    convert_element_type x1, other arithmetic, body(): return (own.astype(full) + other.astype(full)).astype(low)  2.12 us

profile of v3, /device:TPU:1, one launch (start us, length us, event | category | flops | bytes accessed | tf_op | source)
XLA Modules:
  0.0 64.1 jit_solution(8566119056815344985)
XLA Ops:
  0.0 61.9 %shard_map.109 = (bf16[1024,256]{1,0:T(8,128)(2,1)}, bf16[1024,256]{1,0:T(8,128)(2,1)}) custom-call(bf16[128,8,256]{2,1,0:T(8,128)(2,1)} %bitcast.5, bf16[64,2,8,256]{3,2,1,0:T(8,128)(2,1)} %bitcast.6, bf16[64,2,8,256]{3,2,1,0:T(8,128)(2,1)} %bitcast.7, bf16[64,2,8,256]{3,2,1,0:T(8,128)(2,1)} %bitcast.8, f32[8,128]{1,0:T(8,128)} %bitcast.9, ...), custom_call_target="tpu_custom_call" | custom-call | tf_op jit(solution)/shard_map/pallas_call | solution.py:421
  61.9 2.1 %add_convert_fusion = bf16[1024,256]{1,0:T(8,128)(2,1)} fusion(bf16[1024,256]{1,0:T(8,128)(2,1)} %get-tuple-element.8, bf16[1024,256]{1,0:T(8,128)(2,1)} %get-tuple-element.7), kind=kLoop, calls=%fused_computation | loop fusion | flops 1048576 | bytes 1572864 | tf_op jit(solution)/shard_map/convert_element_type | solution.py:477

commit v4 on v3

--- a/solution.py
+++ b/solution.py
@@ -42,6 +42,30 @@
     halves = (high, 32 - high)
     for dz, dy, dx in ORDER:
         act(halves[dy] + far[dz] + near[dx])
+
+
+def every_peer_root_first(me, act):
+    high, z, x = me // 32, (me // 4) % 8, me % 4
+    near = [(x + step) % 4 for step in range(4)]
+    far = [(z + step) % 8 for step in range(8)]
+    halves = (high, 1 - high)
+    for first_z in (0, 7, 1):
+        for first_x in (0, 3, 1):
+            target = first_z * 4 + first_x
+
+            @pl.when(target != me)
+            def _(target=target):
+                act(target)
+
+    z_first = [(place + 1) % 8 <= 2 for place in far]
+    x_first = [(place + 1) % 4 <= 2 for place in near]
+    y_first = [place == 0 for place in halves]
+    for dz, dy, dx in ORDER:
+        first = jnp.logical_and(jnp.logical_and(z_first[dz], x_first[dx]), y_first[dy])
+
+        @pl.when(jnp.logical_not(first))
+        def _(dz=dz, dy=dy, dx=dx):
+            act(halves[dy] * 32 + far[dz] * 4 + near[dx])
 
 
 ORDER = [(4, 1, 2), (3, 1, 2), (4, 1, 1), (4, 1, 3), (5, 1, 2), (2, 1, 2), (3, 1, 1), (3, 1, 3), (4, 0, 2), (4, 1, 0), (5, 1, 1), (5, 1, 3), (6, 1, 2), (1, 1, 2), (2, 1, 1), (2, 1, 3), (3, 0, 2), (3, 1, 0), (4, 0, 1), (4, 0, 3), (5, 0, 2), (5, 1, 0), (6, 1, 1), (6, 1, 3), (7, 1, 2), (0, 1, 2), (1, 1, 1), (1, 1, 3), (2, 0, 2), (2, 1, 0), (3, 0, 1), (3, 0, 3), (4, 0, 0), (5, 0, 1), (5, 0, 3), (6, 0, 2), (6, 1, 0), (7, 1, 1), (7, 1, 3), (0, 1, 1), (0, 1, 3), (1, 0, 2), (1, 1, 0), (2, 0, 1), (2, 0, 3), (3, 0, 0), (5, 0, 0), (6, 0, 1), (6, 0, 3), (7, 0, 2), (7, 1, 0), (0, 0, 2), (0, 1, 0), (1, 0, 1), (1, 0, 3), (2, 0, 0), (6, 0, 0), (7, 0, 1), (7, 0, 3), (0, 0, 1), (0, 0, 3), (1, 0, 0), (7, 0, 0)]
@@ -93,6 +117,8 @@
     first_back_ref,
     twist_ref,
     load_sem,
+    taps_send_sem,
+    taps_recv_sem,
     in_send_sem,
     in_recv_sem,
     back_send_sem,
@@ -157,41 +183,59 @@
                 rows = rows.astype(jnp.float32).reshape(128, 128)
                 skipped[half, part * 128 : part * 128 + 128, :] = spread * rows
 
-    def sent_in(chunk, which, target):
-        source, landing = ((taps, in_taps), (mixed, in_mixed))[which]
-        return pltpu.make_async_remote_copy(
-            src_ref=source.at[target, chunk],
-            dst_ref=landing.at[chunk, me],
-            send_sem=in_send_sem.at[chunk, which],
-            recv_sem=in_recv_sem.at[chunk, which],
+    def sent_taps(target, landing):
+        return pltpu.make_async_remote_copy(
+            src_ref=taps.at[target],
+            dst_ref=in_taps.at[landing],
+            send_sem=taps_send_sem,
+            recv_sem=taps_recv_sem,
             device_id={"ctx": target},
             device_id_type=MESH,
         )
 
-    def push_in(chunk, which):
-        every_peer(me, lambda other: sent_in(chunk, which, other).start())
-        source, landing = ((taps, in_taps), (mixed, in_mixed))[which]
-        landing[chunk, me] = source[me, chunk]
-
-    def wait_in(chunk, which, receive):
-        source, landing = ((taps, in_taps), (mixed, in_mixed))[which]
-        whole = landing.at[chunk, pl.ds(0, CTX - 1)]
-        copy = pltpu.make_async_remote_copy(
+    def sent_mixed(chunk, target):
+        return pltpu.make_async_remote_copy(
+            src_ref=mixed.at[target, chunk],
+            dst_ref=in_mixed.at[chunk, me],
+            send_sem=in_send_sem.at[chunk],
+            recv_sem=in_recv_sem.at[chunk],
+            device_id={"ctx": target},
+            device_id_type=MESH,
+        )
+
+    def push_taps():
+        every_peer(me, lambda other: sent_taps(other, me).start())
+        in_taps[me] = taps[me]
+
+    def push_mixed(chunk):
+        every_peer(me, lambda other: sent_mixed(chunk, other).start())
+        in_mixed[chunk, me] = mixed[me, chunk]
+
+    def all_taps():
+        whole = in_taps.at[pl.ds(0, CTX - 1)]
+        return pltpu.make_async_remote_copy(
             src_ref=whole,
             dst_ref=whole,
-            send_sem=in_send_sem.at[chunk, which],
-            recv_sem=in_recv_sem.at[chunk, which],
+            send_sem=taps_send_sem,
+            recv_sem=taps_recv_sem,
             device_id={"ctx": (me + 1) % CTX},
             device_id_type=MESH,
         )
-        if receive:
-            copy.wait_recv()
-        else:
-            copy.wait_send()
-
-    def spread(chunk, landing, stage):
+
+    def all_mixed(chunk):
+        whole = in_mixed.at[chunk, pl.ds(0, CTX - 1)]
+        return pltpu.make_async_remote_copy(
+            src_ref=whole,
+            dst_ref=whole,
+            send_sem=in_send_sem.at[chunk],
+            recv_sem=in_recv_sem.at[chunk],
+            device_id={"ctx": (me + 1) % CTX},
+            device_id_type=MESH,
+        )
+
+    def spread(take, stage):
         def step(row, carry):
-            block = landing[chunk, row].astype(jnp.float32)
+            block = take(row).astype(jnp.float32)
             stage[row, 0] = block[:, :128]
             stage[row, 1] = block[:, 128:]
             return carry
@@ -215,7 +259,7 @@
         return dot(jnp.concatenate(turned, 0), second_ref[...])
 
     def transform_taps(chunk):
-        spread(chunk, in_taps, stage_taps)
+        spread(lambda row: in_taps[row, chunk], stage_taps)
         for start in range(0, GROUP, SPAN):
             spectra_taps[chunk, start * BASE : (start + SPAN) * BASE, :] = transform(
                 stage_taps, start
@@ -223,7 +267,7 @@
 
     def convolve(chunk):
         cos, sin = twist_ref[0], twist_ref[1]
-        spread(chunk, in_mixed, stage_mixed)
+        spread(lambda row: in_mixed[chunk, row], stage_mixed)
         flat = stage_out.reshape(BASE * GROUP, BASE)
         for start in range(0, GROUP, SPAN):
             right = transform(stage_mixed, start)
@@ -250,58 +294,60 @@
 
         def gather(row, carry):
             for half in range(2):
-                back_send[half, chunk, row] = stage_out[row, half].astype(jnp.bfloat16)
+                back_send[half, row, chunk] = stage_out[row, half].astype(jnp.bfloat16)
             return carry
 
         lax.fori_loop(0, CTX, gather, 0, unroll=8)
         for half in range(2):
-            back_recv[half, me * CHUNKS + chunk] = back_send[half, chunk, me]
-
-    def push_back(half, chunk):
+            back_recv[half, me, chunk] = back_send[half, me, chunk]
+
+    def push_back(half, chunks):
         def send(target):
             pltpu.make_async_remote_copy(
-                src_ref=back_send.at[half, chunk, target],
-                dst_ref=back_recv.at[half, me * CHUNKS + chunk],
+                src_ref=back_send.at[half, target, chunks],
+                dst_ref=back_recv.at[half, me, chunks],
                 send_sem=back_send_sem.at[half],
                 recv_sem=back_recv_sem.at[half],
                 device_id={"ctx": target},
                 device_id_type=MESH,
             ).start()
 
-        every_peer(me, send)
-
+        every_peer_root_first(me, send)
+
+    first_chunk, last_chunk, both_chunks = pl.ds(0, 1), pl.ds(1, 1), pl.ds(0, 2)
     loads[0].wait()
     pl.semaphore_wait(barrier, CTX + 1)
-    push_in(0, 0)
-    push_in(1, 0)
+    push_taps()
     loads[1].wait()
     loads[2].wait()
     multiply(0)
-    push_in(0, 1)
+    push_mixed(0)
     multiply(1)
-    push_in(1, 1)
+    push_mixed(1)
     for load in loads[3:9]:
         load.wait()
     skip()
-    wait_in(0, 0, True)
+    all_taps().wait_recv()
     transform_taps(0)
-    wait_in(1, 0, True)
     transform_taps(1)
-    wait_in(0, 1, True)
+    all_mixed(0).wait_recv()
     convolve(0)
-    push_back(0, 0)
-    wait_in(1, 1, True)
+    push_back(0, first_chunk)
+    all_mixed(1).wait_recv()
     convolve(1)
-    push_back(0, 1)
-    push_back(1, 0)
+    push_back(0, last_chunk)
 
     @pl.when(core == 0)
     def _():
-        push_back(1, 1)
+        push_back(1, both_chunks)
+
+    @pl.when(core == 1)
+    def _():
+        push_back(1, first_chunk)
 
 
     def wait_back(half):
-        whole = back_recv.at[half, pl.ds(0, (CTX - 1) * CHUNKS)]
+        whole = back_recv.at[half, pl.ds(0, CTX - 1)]
         return pltpu.make_async_remote_copy(
             src_ref=whole,
             dst_ref=whole,
@@ -343,7 +389,7 @@
         for part in range(8):
             lanes = slice(half * 128, half * 128 + 128)
             block = slice(part * 16, part * 16 + 16)
-            conv = back_recv[half, block].astype(jnp.float32).reshape(128, 128)
+            conv = back_recv[half, part * 8 : part * 8 + 8].astype(jnp.float32).reshape(128, 128)
             gates = gate[block, :, lanes].astype(jnp.float32).reshape(128, 128)
             rows = slice(part * 128, part * 128 + 128)
             gated[half, rows, :] = (gates * (conv + skipped[half, rows, :])).astype(jnp.bfloat16)
@@ -385,12 +431,12 @@
         return lambda: combine(PIECES - 1)
 
     wait_back(0).wait_recv()
-    gating(0)
 
     @pl.when(core == 1)
     def _():
-        push_back(1, 1)
-
+        push_back(1, last_chunk)
+
+    gating(0)
     sums(0, 0)()
     wait_back(1).wait_recv()
     gating(1)
@@ -400,9 +446,9 @@
     sums(1, 1)()
     own_out(1).start()
 
+    all_taps().wait_send()
     for chunk in range(CHUNKS):
-        wait_in(chunk, 0, False)
-        wait_in(chunk, 1, False)
+        all_mixed(chunk).wait_send()
     for half in range(2):
         wait_back(half).wait_send()
         for slot in range(2):
@@ -432,13 +478,13 @@
             pltpu.VMEM(messages, low),
             pltpu.VMEM((2, 1024, 128), full),
             pltpu.VMEM((CHUNKS, CTX, GROUP, 256), low),
-            pltpu.VMEM((CHUNKS, CTX, GROUP, 256), low),
+            pltpu.VMEM(messages, low),
             pltpu.VMEM((CTX, 2, GROUP, 128), full),
             pltpu.VMEM((CTX, 2, GROUP, 128), full),
             pltpu.VMEM((CTX, 2, GROUP, 128), full),
             pltpu.VMEM((CHUNKS, GROUP * BASE, 2 * BASE), full),
-            pltpu.VMEM((2, CHUNKS, CTX, GROUP, 128), low),
-            pltpu.VMEM((2, CTX * CHUNKS, GROUP, 128), low),
+            pltpu.VMEM((2, CTX, CHUNKS, GROUP, 128), low),
+            pltpu.VMEM((2, CTX, CHUNKS, GROUP, 128), low),
             pltpu.VMEM((2, 1024, 128), low),
             pltpu.VMEM((2, 2, 1024, 128), low),
             pltpu.VMEM((2, 2, 1024, 128), low),
@@ -452,8 +498,10 @@
             pltpu.VMEM((BASE, 2 * BASE), low),
             pltpu.VMEM((2, BASE, BASE), full),
             dma((11,)),
-            dma((CHUNKS, 2)),
-            dma((CHUNKS, 2)),
+            dma(()),
+            dma(()),
+            dma((CHUNKS,)),
+            dma((CHUNKS,)),
             dma((2,)),
             dma((2,)),
             dma((2, 2, PIECES)),

time: 64.2 us -> 64 us (level)
  no operation moved by 1% of the time
where the time goes in v4:
time: 64 us; the launch traced here: 63.9 us
  Pallas kernels  61.7 us (96%)
  other arithmetic  2.12 us (3%)
    pallas_call x1, Pallas kernels, body(): pl.pallas_call(kernel, out_shape=[jax.ShapeDtypeStruct((1024, 256), low)]...  61.7 us
    convert_element_type x1, other arithmetic, body(): return (own.astype(full) + other.astype(full)).astype(low)  2.12 us

profile of v4, /device:TPU:1, one launch (start us, length us, event | category | flops | bytes accessed | tf_op | source)
XLA Modules:
  0.0 63.9 jit_solution(10480265982842602379)
XLA Ops:
  0.0 61.7 %shard_map.109 = (bf16[1024,256]{1,0:T(8,128)(2,1)}, bf16[1024,256]{1,0:T(8,128)(2,1)}) custom-call(bf16[128,8,256]{2,1,0:T(8,128)(2,1)} %bitcast.5, bf16[64,2,8,256]{3,2,1,0:T(8,128)(2,1)} %bitcast.6, bf16[64,2,8,256]{3,2,1,0:T(8,128)(2,1)} %bitcast.7, bf16[64,2,8,256]{3,2,1,0:T(8,128)(2,1)} %bitcast.8, f32[8,128]{1,0:T(8,128)} %bitcast.9, ...), custom_call_target="tpu_custom_call" | custom-call | tf_op jit(solution)/shard_map/pallas_call | solution.py:467
  61.7 2.1 %add_convert_fusion = bf16[1024,256]{1,0:T(8,128)(2,1)} fusion(bf16[1024,256]{1,0:T(8,128)(2,1)} %get-tuple-element.8, bf16[1024,256]{1,0:T(8,128)(2,1)} %get-tuple-element.7), kind=kLoop, calls=%fused_computation | loop fusion | flops 1048576 | bytes 1572864 | tf_op jit(solution)/shard_map/convert_element_type | solution.py:525
